TPU v7x, 32 devices: a whole 2x2x4 slice. The times are simulated.
32 devices in a mesh: src: 8 (over z, x), rcv: 4 (over y, core).
Axes of the slice: x: 2, y: 2, z: 4, core: 2. Of those that a mesh axis runs over, the one named last changes fastest.
Arguments:
- traces: bfloat16 [2, 2, 2048, 2048], P(None, None, 'src', 'rcv'), may hold values from -8 to 8
- wavelet: float32 [2, 2], replicated, may hold values from -0.3 to 0.3
Outputs:
- coeffs: float32 [2, 2, 2048, 2048], P(None, None, 'src', 'rcv')
- norms: float32 [2, 2], replicated
All inputs are finite; a program needn't handle non-finite values.
Results may differ from a plain program's by a relative error of at most 0.006.
Values may be sent and summed in bfloat16 or wider, within the bound.
A program may use at most 128 MiB of HBM per device.

v0:
```python
import math
import jax
import jax.numpy as jnp
from jax import lax
from jax.sharding import PartitionSpec as P

ITERS = 2
step_length = 0.4
shrink_fraction = 0.2


def table_block(offset, height, second, breadth, length, direction):
    left_index = offset + jnp.arange(height, dtype=jnp.int32)
    right_index = second + jnp.arange(breadth, dtype=jnp.int32)
    phase = left_index[:, None] * right_index[None, :] % length
    angle = phase.astype(jnp.float32) * (2.0 * math.pi / length)
    scale = 1.0 / math.sqrt(length)
    return jnp.stack([jnp.cos(angle) * scale, direction * (jnp.sin(angle) * scale)]).astype(
        jnp.bfloat16
    )


def complex_product(left_side, right_side, pattern, left_table, right_table):
    left_re = left_side[0] if left_table else left_side[:, 0]
    left_im = left_side[1] if left_table else left_side[:, 1]
    right_re = right_side[0] if right_table else right_side[:, 0]
    right_im = right_side[1] if right_table else right_side[:, 1]

    def single(first_op, second_op):
        return jnp.einsum(pattern, first_op, second_op, preferred_element_type=jnp.float32)

    real_part = single(left_re, right_re) - single(left_im, right_im)
    imag_part = single(left_re, right_im) + single(left_im, right_re)
    return jnp.stack([real_part, imag_part], axis=1)


def complex_scale(real_part, imag_part, values):
    return jnp.stack(
        [
            real_part * values[:, 0] - imag_part * values[:, 1],
            real_part * values[:, 1] + imag_part * values[:, 0],
        ],
        axis=1,
    )


def per_device(traces, wavelet):
    row_count = traces.shape[2]
    col_count = traces.shape[3]
    extent = row_count * lax.axis_size("src")
    row_anchor = lax.axis_index("src") * row_count
    col_anchor = lax.axis_index("rcv") * col_count
    root_scale = 1.0 / math.sqrt(extent)
    wave_re = (wavelet[:, 0] * root_scale)[:, None, None]
    wave_im = (wavelet[:, 1] * root_scale)[:, None, None]
    forward_cols = table_block(0, extent, col_anchor, col_count, extent, -1.0)
    forward_rows = table_block(row_anchor, row_count, 0, extent, extent, -1.0)
    inverse_cols = table_block(0, extent, col_anchor, col_count, extent, 1.0)
    inverse_rows = table_block(row_anchor, row_count, 0, extent, extent, 1.0)
    coeffs = jnp.zeros(traces.shape, jnp.float32)
    columns_all = lax.all_gather(traces, "src", axis=2, tiled=True)
    traces_f = traces.astype(jnp.float32)

    def row_section(table, portion):
        return complex_product(portion, table, "fmn,nc->fmc", False, True)

    def column_section(table, portion):
        return complex_product(table, portion, "mn,fnc->fmc", True, False)

    def paired(first_op, second_op):
        return jnp.einsum("fmr,fkr->fmk", first_op, second_op, preferred_element_type=jnp.float32)

    norm_list = []
    for iteration in range(ITERS):
        if iteration == 0:
            misfit = traces_f
        else:
            coeff_half = coeffs.astype(jnp.bfloat16)
            halfway = column_section(
                inverse_rows, lax.all_gather(coeff_half, "src", axis=2, tiled=True)
            ).astype(jnp.bfloat16)
            model = row_section(
                inverse_cols, lax.all_gather(halfway, "rcv", axis=3, tiled=True)
            ).astype(jnp.bfloat16)
            product = complex_product(
                lax.all_gather(model, "rcv", axis=3, tiled=True),
                columns_all,
                "fmn,fnc->fmc",
                False,
                False,
            )
            misfit = traces_f - model.astype(jnp.float32) + complex_scale(wave_re, wave_im, product)
        local_squares = jnp.sum(misfit * misfit, axis=(1, 2, 3))
        norm_list.append(jnp.sqrt(lax.psum(local_squares, ("src", "rcv"))))
        misfit_half = misfit.astype(jnp.bfloat16)
        misfit_re = misfit_half[:, 0]
        misfit_im = misfit_half[:, 1]
        column_re = columns_all[:, 0]
        column_im = columns_all[:, 1]
        back_re = paired(misfit_re, column_re) + paired(misfit_im, column_re * 0 + column_im)
        back_im = paired(misfit_im, column_re) - paired(misfit_re, column_im)
        scaled = complex_scale(wave_re, -wave_im, jnp.stack([back_re, back_im], axis=1))
        summed = lax.psum_scatter(
            scaled.astype(jnp.bfloat16), "rcv", scatter_dimension=3, tiled=True
        ).astype(jnp.float32)
        grad_half = (misfit_half.astype(jnp.float32) - summed).astype(jnp.bfloat16)
        halfway = row_section(
            forward_cols, lax.all_gather(grad_half, "rcv", axis=3, tiled=True)
        ).astype(jnp.bfloat16)
        spectrum = column_section(forward_rows, lax.all_gather(halfway, "src", axis=2, tiled=True))
        trial = coeffs + step_length * spectrum
        magnitude = jnp.sqrt(trial[:, 0] * trial[:, 0] + trial[:, 1] * trial[:, 1])
        local_peak = jnp.max(magnitude, axis=(1, 2))
        global_peak = lax.pmax(local_peak, ("src", "rcv"))
        level = shrink_fraction * global_peak[:, None, None]
        factor = jnp.maximum(1.0 - level / jnp.maximum(magnitude, level), 0.0)
        coeffs = trial * factor[:, None]
    return (coeffs, jnp.stack(norm_list))


def solution(mesh):
    in_specs = (P(None, None, "src", "rcv"), P())
    out_specs = (P(None, None, "src", "rcv"), P())
    return jax.shard_map(
        per_device, mesh=mesh, in_specs=in_specs, out_specs=out_specs, check_vma=False
    )
```

profile of v0, /device:TPU:0, one launch (start us, length us, event | category | flops | bytes accessed | tf_op | source)
XLA Modules:
  0.0 1197.7 jit_solution(8126801174571797452)
XLA Ops:
  7.2 2.3 copy.4
  9.6 1.0 multiply_reduce_fusion.2
  10.5 127.4 %all-gather.9.cloned.1.call-done = bf16[2,2,2048,512]{3,2,0,1:T(8,128)(2,1)} async-done(((bf16[2,2,256,512]{3,2,0,1:T(8,128)(2,1)}), bf16[2,2,2048,512]{3,2,0,1:T(8,128)(2,1)}) %all-gather.9.cloned.1.call-update) | async-done | bytes 8388624 | tf_op jit(solution)/shard_map/all_gather | solution.py:61
  137.9 3.8 fusion.137
  141.7 1.0 copy-done
  142.7 3.3 fusion.138
  146.0 3.3 bitcast_add_fusion
  149.3 1.9 fusion.26
  151.2 2.3 pad_maximum_fusion
  153.7 42.7 %reduce-scatter.3.cloned.1.call-done = bf16[2,2,256,512]{3,2,0,1:T(8,128)(2,1)} async-done(((bf16[2,2,256,2048]{3,2,0,1:T(8,128)(2,1)}), bf16[2,2,256,512]{3,2,0,1:T(8,128)(2,1)}) %reduce-scatter.3.cloned.1.call-update) | async-done | bytes 1048592 | tf_op jit(solution)/shard_map/reduce_scatter | solution.py:103
  196.4 2.5 fusion.20
  199.4 34.1 %all-gather.11.cloned.1.call-done = bf16[2,2,256,2048]{3,2,0,1:T(8,128)(2,1)} async-done(((bf16[2,2,256,512]{3,2,0,1:T(8,128)(2,1)}), bf16[2,2,256,2048]{3,2,0,1:T(8,128)(2,1)}) %all-gather.11.cloned.1.call-update) | async-done | bytes 4194320 | tf_op jit(solution)/shard_map/all_gather | solution.py:108
  233.5 17.6 %fusion.45 = f32[2,256,512]{2,1,0:T(8,128)S(1)} fusion(s32[512]{0:T(512)S(1)} %iota_add_fusion, bf16[2,2,256,2048]{3,2,0,1:T(8,128)(2,1)} %all-gather.11.cloned.1.call-done), kind=kOutput, calls=%fused_computation.87 | convolution fusion | flops 1090519040 | bytes 3147776 | tf_op jit(solution)/shard_map/fmn,nc->fmc/dot_general | solution.py:30
  251.1 15.9 %fusion.47 = f32[2,256,512]{2,1,0:T(8,128)S(1)} fusion(s32[512]{0:T(512)S(1)} %iota_add_fusion, bf16[2,2,256,2048]{3,2,0,1:T(8,128)(2,1)S(1)} %copy-done.13), kind=kOutput, calls=%fused_computation.88 | convolution fusion | flops 1090519040 | bytes 3147776 | tf_op jit(solution)/shard_map/fmn,nc->fmc/dot_general | solution.py:30
  266.9 16.4 %fusion.124 = bf16[2,1,256,512]{3,2,0,1:T(8,128)(2,1)S(1)} fusion(f32[2,256,512]{2,1,0:T(8,128)S(1)} %fusion.45, s32[512]{0:T(512)S(1)} %iota_add_fusion, bf16[2,2,256,2048]{3,2,0,1:T(8,128)(2,1)S(1)} %copy-done.13), kind=kOutput, calls=%fused_computation.129 | convolution fusion | flops 1091043328 | bytes 3672064 | tf_op jit(solution)/shard_map/fmn,nc->fmc/dot_general | solution.py:30
  283.3 16.6 %fusion.121 = bf16[2,1,256,512]{3,2,0,1:T(8,128)(2,1)S(1)} fusion(f32[2,256,512]{2,1,0:T(8,128)S(1)} %fusion.47, s32[512]{0:T(512)S(1)} %iota_add_fusion, bf16[2,2,256,2048]{3,2,0,1:T(8,128)(2,1)S(1)} %copy-done.13), kind=kOutput, calls=%fused_computation.128 | convolution fusion | flops 1091043328 | bytes 3672064 | tf_op jit(solution)/shard_map/fmn,nc->fmc/dot_general | solution.py:30
  299.9 1.1 pad_maximum_fusion.3
  301.1 124.5 %all-gather.13.cloned.1.call-done = bf16[2,2,2048,512]{3,2,0,1:T(8,128)(2,1)} async-done(((bf16[2,2,256,512]{3,2,0,1:T(8,128)(2,1)}), bf16[2,2,2048,512]{3,2,0,1:T(8,128)(2,1)}) %all-gather.13.cloned.1.call-update) | async-done | bytes 8388624 | tf_op jit(solution)/shard_map/all_gather | solution.py:110
  425.6 10.8 fusion.6
  436.4 8.5 fusion.7
  444.9 8.7 fusion.92
  453.7 8.4 fusion.90
  463.6 38.3 %pmax.14 = f32[2]{0:T(128)S(1)} all-reduce(f32[2]{0:T(128)S(1)} %fusion.160), channel_id=1, replica_groups=mesh['src'=8,'rcv'=4] {'src','rcv'}, use_global_device_ids=true, to_apply=%region_2.3 | all-reduce | flops 2 | bytes 16 | tf_op jit(solution)/shard_map/pmax | solution.py:114
  502.5 1.0 copy-done.2
  503.4 2.8 multiply_convert_fusion.6
  506.5 125.6 %all-gather.15.cloned.1.call-done = bf16[2,2,2048,512]{2,3,0,1:T(8,128)(2,1)} async-done(((bf16[2,2,256,512]{2,3,0,1:T(8,128)(2,1)}), bf16[2,2,2048,512]{2,3,0,1:T(8,128)(2,1)}) %all-gather.15.cloned.1.call-update) | async-done | bytes 8388624 | tf_op jit(solution)/shard_map/all_gather | solution.py:80
  632.0 11.0 fusion.10
  643.0 8.7 fusion.11
  651.8 9.0 fusion.134
  660.7 8.6 fusion.133
  669.3 1.1 pad_maximum_fusion.4
  670.6 32.6 %all-gather.17.cloned.1.call-done = bf16[2,2,256,2048]{2,3,0,1:T(8,128)(2,1)} async-done(((bf16[2,2,256,512]{2,3,0,1:T(8,128)(2,1)}), bf16[2,2,256,2048]{2,3,0,1:T(8,128)(2,1)}) %all-gather.17.cloned.1.call-update) | async-done | bytes 4194320 | tf_op jit(solution)/shard_map/all_gather | solution.py:83
  703.2 18.5 %fusion.41 = f32[2,256,512]{2,1,0:T(8,128)S(1)} fusion(s32[512]{0:T(512)S(1)} %iota_add_fusion, bf16[2,2,256,2048]{2,3,0,1:T(8,128)(2,1)} %all-gather.17.cloned.1.call-done), kind=kOutput, calls=%fused_computation.85 | convolution fusion | flops 1090519040 | bytes 3147776 | tf_op jit(solution)/shard_map/fmn,nc->fmc/dot_general | solution.py:30
  721.7 16.9 %fusion.43 = f32[2,256,512]{2,1,0:T(8,128)S(1)} fusion(s32[512]{0:T(512)S(1)} %iota_add_fusion, bf16[2,2,256,2048]{2,3,0,1:T(8,128)(2,1)S(1)} %copy-done.16), kind=kOutput, calls=%fused_computation.86 | convolution fusion | flops 1090519040 | bytes 3147776 | tf_op jit(solution)/shard_map/fmn,nc->fmc/dot_general | solution.py:30
  738.6 17.2 %fusion.118 = bf16[2,1,256,512]{3,2,0,1:T(8,128)(2,1)S(1)} fusion(f32[2,256,512]{2,1,0:T(8,128)S(1)} %fusion.41, s32[512]{0:T(512)S(1)} %iota_add_fusion, bf16[2,2,256,2048]{2,3,0,1:T(8,128)(2,1)S(1)} %copy-done.16), kind=kOutput, calls=%fused_computation.127 | convolution fusion | flops 1091043328 | bytes 3672064 | tf_op jit(solution)/shard_map/fmn,nc->fmc/dot_general | solution.py:30
  755.8 16.8 %fusion.115 = bf16[2,1,256,512]{3,2,0,1:T(8,128)(2,1)S(1)} fusion(f32[2,256,512]{2,1,0:T(8,128)S(1)} %fusion.43, s32[512]{0:T(512)S(1)} %iota_add_fusion, bf16[2,2,256,2048]{2,3,0,1:T(8,128)(2,1)S(1)} %copy-done.16), kind=kOutput, calls=%fused_computation.126 | convolution fusion | flops 1091043328 | bytes 3672064 | tf_op jit(solution)/shard_map/fmn,nc->fmc/dot_general | solution.py:30
  772.7 1.1 pad_maximum_fusion.5
  773.8 34.6 %all-gather.19.cloned.1.call-done = bf16[2,2,256,2048]{3,2,0,1:T(8,128)(2,1)} async-done(((bf16[2,2,256,512]{3,2,0,1:T(8,128)(2,1)}), bf16[2,2,256,2048]{3,2,0,1:T(8,128)(2,1)}) %all-gather.19.cloned.1.call-update) | async-done | bytes 4194320 | tf_op jit(solution)/shard_map/all_gather | solution.py:86
  808.4 4.2 fusion.63
  812.6 3.6 fusion.62
  816.2 3.6 fusion.93
  819.8 1.4 subtract_bitcast_fusion
  822.1 1.3 fusion.135
  823.4 1.3 fusion.136
  824.7 1.3 convolution_subtract_fusion
  826.0 3.6 fusion.31
  829.6 4.5 pad_maximum_fusion.1
  834.2 44.5 %reduce-scatter.5.cloned.1.call-done = bf16[2,2,256,512]{3,2,0,1:T(8,128)(2,1)} async-done(((bf16[2,2,256,2048]{3,2,0,1:T(8,128)(2,1)}), bf16[2,2,256,512]{3,2,0,1:T(8,128)(2,1)}) %reduce-scatter.5.cloned.1.call-update) | async-done | bytes 1048592 | tf_op jit(solution)/shard_map/reduce_scatter | solution.py:103
  878.7 2.5 subtract_convert_fusion.2
  881.6 34.2 %all-gather.21.cloned.1.call-done = bf16[2,2,256,2048]{3,2,0,1:T(8,128)(2,1)} async-done(((bf16[2,2,256,512]{3,2,0,1:T(8,128)(2,1)}), bf16[2,2,256,2048]{3,2,0,1:T(8,128)(2,1)}) %all-gather.21.cloned.1.call-update) | async-done | bytes 4194320 | tf_op jit(solution)/shard_map/all_gather | solution.py:108
  915.8 17.6 %fusion.37 = f32[2,256,512]{2,1,0:T(8,128)S(1)} fusion(s32[512]{0:T(512)S(1)} %iota_add_fusion, bf16[2,2,256,2048]{3,2,0,1:T(8,128)(2,1)} %all-gather.21.cloned.1.call-done), kind=kOutput, calls=%fused_computation.83 | convolution fusion | flops 1090519040 | bytes 3147776 | tf_op jit(solution)/shard_map/fmn,nc->fmc/dot_general | solution.py:30
  933.4 15.9 %fusion.39 = f32[2,256,512]{2,1,0:T(8,128)S(1)} fusion(s32[512]{0:T(512)S(1)} %iota_add_fusion, bf16[2,2,256,2048]{3,2,0,1:T(8,128)(2,1)S(1)} %copy-done.15), kind=kOutput, calls=%fused_computation.84 | convolution fusion | flops 1090519040 | bytes 3147776 | tf_op jit(solution)/shard_map/fmn,nc->fmc/dot_general | solution.py:30
  949.2 16.4 %fusion.130 = bf16[2,1,256,512]{3,2,0,1:T(8,128)(2,1)S(1)} fusion(f32[2,256,512]{2,1,0:T(8,128)S(1)} %fusion.37, s32[512]{0:T(512)S(1)} %iota_add_fusion, bf16[2,2,256,2048]{3,2,0,1:T(8,128)(2,1)S(1)} %copy-done.15), kind=kOutput, calls=%fused_computation.131 | convolution fusion | flops 1091043328 | bytes 3672064 | tf_op jit(solution)/shard_map/fmn,nc->fmc/dot_general | solution.py:30
  965.6 17.0 %fusion.127 = bf16[2,1,256,512]{3,2,0,1:T(8,128)(2,1)S(1)} fusion(f32[2,256,512]{2,1,0:T(8,128)S(1)} %fusion.39, s32[512]{0:T(512)S(1)} %iota_add_fusion, bf16[2,2,256,2048]{3,2,0,1:T(8,128)(2,1)S(1)} %copy-done.15), kind=kOutput, calls=%fused_computation.130 | convolution fusion | flops 1091043328 | bytes 3672064 | tf_op jit(solution)/shard_map/fmn,nc->fmc/dot_general | solution.py:30
  982.7 1.1 pad_maximum_fusion.6
  983.8 42.2 %all-reduce = (f32[2]{0:T(128)S(1)}, f32[2]{0:T(128)S(1)}) all-reduce(f32[2]{0:T(128)S(1)} %get-tuple-element.5, f32[2]{0:T(128)S(1)} %get-tuple-element.4), channel_id=1, replica_groups=mesh['src'=8,'rcv'=4] {'src','rcv'}, use_global_device_ids=true, to_apply=%region_9.10 | all-reduce | flops 4 | bytes 32 | tf_op jit(solution)/shard_map/psum | solution.py:94
  1025.9 83.5 %all-gather.23.cloned.1.call-done = bf16[2,2,2048,512]{3,2,0,1:T(8,128)(2,1)} async-done(((bf16[2,2,256,512]{3,2,0,1:T(8,128)(2,1)}), bf16[2,2,2048,512]{3,2,0,1:T(8,128)(2,1)}) %all-gather.23.cloned.1.call-update) | async-done | bytes 8388624 | tf_op jit(solution)/shard_map/all_gather | solution.py:110
  1109.4 10.8 fusion.14
  1120.2 8.5 fusion.15
  1128.7 8.6 fusion.86
  1137.3 8.4 fusion.84
  1147.4 38.3 %pmax.15 = f32[2]{0:T(128)S(1)} all-reduce(f32[2]{0:T(128)S(1)} %fusion.161), channel_id=1, replica_groups=mesh['src'=8,'rcv'=4] {'src','rcv'}, use_global_device_ids=true, to_apply=%region_5.6 | all-reduce | flops 2 | bytes 16 | tf_op jit(solution)/shard_map/pmax | solution.py:114
  1186.2 2.6 broadcast_multiply_fusion
  1188.8 1.8 copy.21
  (71 shorter events, 6.8 us)
Async XLA Ops:
  7.2 130.8 %all-gather.9.cloned.1.call-start = ((), (), s32[]{:S(2)}) async-start(), calls=%async_computation.2 | async-start | bytes 9437184 | tf_op jit(solution)/shard_map/all_gather | solution.py:61
  9.5 132.3 %copy-start.1 = (bf16[2,2,256,512]{3,2,1,0:T(8,128)(2,1)S(1)}, bf16[2,2,256,512]{3,2,1,0:T(8,128)(2,1)}, u32[]{:S(2)}) copy-start(bf16[2,2,256,512]{3,2,1,0:T(8,128)(2,1)} %param.2) | copy-start | bytes 3145732
  9.5 186.9 %reduce-scatter.3.cloned.1.call-start = ((), (), s32[]{:S(2)}) async-start(), calls=%async_computation.3 | async-start | bytes 5242880 | tf_op jit(solution)/shard_map/reduce_scatter | solution.py:103
  137.9 4.8 copy-start
  153.6 79.9 %all-gather.11.cloned.1.call-start = ((), (), s32[]{:S(2)}) async-start(), calls=%async_computation.4 | async-start | bytes 5242880 | tf_op jit(solution)/shard_map/all_gather | solution.py:108
  198.9 226.7 %all-gather.13.cloned.1.call-start = ((), (), s32[]{:S(2)}) async-start(), calls=%async_computation.5 | async-start | bytes 9437184 | tf_op jit(solution)/shard_map/all_gather | solution.py:110
  233.5 17.6 %copy-start.13 = (bf16[2,2,256,2048]{3,2,0,1:T(8,128)(2,1)S(1)}, bf16[2,2,256,2048]{3,2,0,1:T(8,128)(2,1)}, u32[]{:S(2)}) copy-start(bf16[2,2,256,2048]{3,2,0,1:T(8,128)(2,1)} %all-gather.11.cloned.1.call-done) | copy-start | bytes 12582916
  301.0 331.0 %all-gather.15.cloned.1.call-start = ((), (), s32[]{:S(2)}) async-start(), calls=%async_computation.6 | async-start | bytes 9437184 | tf_op jit(solution)/shard_map/all_gather | solution.py:80
  425.6 10.8 copy-start.10
  453.7 8.4 copy-start.4
  462.1 1.0 copy-start.6
  502.4 1.0 copy-start.2
  506.2 197.0 %all-gather.17.cloned.1.call-start = ((), (), s32[]{:S(2)}) async-start(), calls=%async_computation.7 | async-start | bytes 5242880 | tf_op jit(solution)/shard_map/all_gather | solution.py:83
  632.0 11.0 copy-start.12
  670.4 138.0 %all-gather.19.cloned.1.call-start = ((), (), s32[]{:S(2)}) async-start(), calls=%async_computation.8 | async-start | bytes 5242880 | tf_op jit(solution)/shard_map/all_gather | solution.py:86
  703.2 18.5 %copy-start.16 = (bf16[2,2,256,2048]{2,3,0,1:T(8,128)(2,1)S(1)}, bf16[2,2,256,2048]{2,3,0,1:T(8,128)(2,1)}, u32[]{:S(2)}) copy-start(bf16[2,2,256,2048]{2,3,0,1:T(8,128)(2,1)} %all-gather.17.cloned.1.call-done) | copy-start | bytes 12582916
  773.8 104.9 %reduce-scatter.5.cloned.1.call-start = ((), (), s32[]{:S(2)}) async-start(), calls=%async_computation.9 | async-start | bytes 5242880 | tf_op jit(solution)/shard_map/reduce_scatter | solution.py:103
  808.4 4.2 copy-start.14
  812.6 7.2 slice-start
  816.2 3.6 slice-start.1
  834.1 81.7 %all-gather.21.cloned.1.call-start = ((), (), s32[]{:S(2)}) async-start(), calls=%async_computation.10 | async-start | bytes 5242880 | tf_op jit(solution)/shard_map/all_gather | solution.py:108
  881.2 228.2 %all-gather.23.cloned.1.call-start = ((), (), s32[]{:S(2)}) async-start(), calls=%async_computation.11 | async-start | bytes 9437184 | tf_op jit(solution)/shard_map/all_gather | solution.py:110
  915.8 17.6 %copy-start.15 = (bf16[2,2,256,2048]{3,2,0,1:T(8,128)(2,1)S(1)}, bf16[2,2,256,2048]{3,2,0,1:T(8,128)(2,1)}, u32[]{:S(2)}) copy-start(bf16[2,2,256,2048]{3,2,0,1:T(8,128)(2,1)} %all-gather.21.cloned.1.call-done) | copy-start | bytes 12582916
  1109.4 10.8 copy-start.11
  1137.3 8.5 copy-start.8
  1137.3 8.5 copy-start.3
  1137.3 8.5 copy-start.5
  1137.3 8.5 copy-start.7
  1145.8 1.0 copy-start.9
Sparse Core Ops, SparseCore 0:
  10.7 127.1 all-gather.8
  153.7 42.5 reduce-scatter.2
  199.0 34.4 all-gather.10
  301.1 124.4 all-gather.12
  506.4 125.6 all-gather.14
  670.5 32.6 all-gather.16
  773.9 34.4 all-gather.18
  834.3 44.3 reduce-scatter.4
  881.3 34.4 all-gather.20
  983.9 125.4 all-gather.22
where the time goes:
time: 1200 us
  waiting for transfers between devices  684 us (57%)
  matrix products  345 us (29%)
  blocking collectives  119 us (10%)
  other arithmetic  26.4 us (2%)
  between operations  14.9 us (1%)
    dot_general x28, matrix products, single(): jnp.einsum(pattern, first_op, second_op, preferred_element_type=jnp.float32)  325 us
    all_gather x2, waiting for transfers between devices, per_device(): lax.all_gather(halfway, 'src', axis=2, tiled=True)  208 us
    all_gather x1, waiting for transfers between devices, per_device(): columns_all = lax.all_gather(traces, 'src', axis=2, tiled=True)  127 us
    all_gather x1, waiting for transfers between devices, per_device(): lax.all_gather(coeff_half, 'src', axis=2, tiled=True)  126 us
    reduce_scatter x2, waiting for transfers between devices, per_device(): lax.psum_scatter(scaled.astype(jnp.bfloat16), 'rcv', scatter_dimension=3,...  87.2 us
    pmax x2, blocking collectives, per_device(): global_peak = lax.pmax(local_peak, ('src', 'rcv'))  76.6 us
    all_gather x2, waiting for transfers between devices, per_device(): lax.all_gather(grad_half, 'rcv', axis=3, tiled=True)  68.3 us
    psum x1, blocking collectives, per_device(): norm_list.append(jnp.sqrt(lax.psum(local_squares, ('src', 'rcv'))))  42.2 us
  transfers between devices with their start and end apart: 10, of which 10 were waited for; matrix products, arithmetic and copies ran while one was open for 0% of the time, Pallas kernels for 0%

commit v1 on v0

--- a/solution.py
+++ b/solution.py
@@ -58,7 +58,7 @@
     inverse_cols = table_block(0, extent, col_anchor, col_count, extent, 1.0)
     inverse_rows = table_block(row_anchor, row_count, 0, extent, extent, 1.0)
     coeffs = jnp.zeros(traces.shape, jnp.float32)
-    columns_all = lax.all_gather(traces, "src", axis=2, tiled=True)
+    columns_all = jnp.concatenate(lax.all_gather(traces, "src"), axis=2)
     traces_f = traces.astype(jnp.float32)
 
     def row_section(table, portion):

time: 1200 us -> 1210 us (level)
  no operation moved by 1% of the time
where the time goes in v1:
time: 1210 us; the launch traced here: 1200 us
  waiting for transfers between devices  685 us (57%)
  matrix products  345 us (29%)
  blocking collectives  119 us (10%)
  other arithmetic  24.5 us (2%)
  between operations  14.8 us (1%)
  local copies, waits for them, and re-layouts  12.6 us (1%)
    dot_general x28, matrix products, single(): jnp.einsum(pattern, first_op, second_op, preferred_element_type=jnp.float32)  323 us
    all_gather x2, waiting for transfers between devices, per_device(): lax.all_gather(halfway, 'src', axis=2, tiled=True)  208 us
    all_gather x1, waiting for transfers between devices, per_device(): columns_all = jnp.concatenate(lax.all_gather(traces, 'src'), axis=2)  128 us
    all_gather x1, waiting for transfers between devices, per_device(): lax.all_gather(coeff_half, 'src', axis=2, tiled=True)  126 us
    reduce_scatter x2, waiting for transfers between devices, per_device(): lax.psum_scatter(scaled.astype(jnp.bfloat16), 'rcv', scatter_dimension=3,...  87.2 us
    pmax x2, blocking collectives, per_device(): global_peak = lax.pmax(local_peak, ('src', 'rcv'))  76.6 us
    all_gather x2, waiting for transfers between devices, per_device(): lax.all_gather(grad_half, 'rcv', axis=3, tiled=True)  68.2 us
    psum x1, blocking collectives, per_device(): norm_list.append(jnp.sqrt(lax.psum(local_squares, ('src', 'rcv'))))  42.2 us
  transfers between devices with their start and end apart: 10, of which 10 were waited for; matrix products, arithmetic and copies ran while one was open for 0% of the time, Pallas kernels for 0%

profile of v1, /device:TPU:0, one launch (start us, length us, event | category | flops | bytes accessed | tf_op | source)
XLA Modules:
  0.0 1202.5 jit_solution(2727884339384674448)
XLA Ops:
  7.9 1.0 multiply_reduce_fusion.2
  8.9 128.4 %all-gather.24.cloned.1.call-done = bf16[16,2,256,512]{3,2,1,0:T(8,128)(2,1)} async-done(((bf16[2,2,256,512]{3,2,1,0:T(8,128)(2,1)}), bf16[16,2,256,512]{3,2,1,0:T(8,128)(2,1)}) %all-gather.24.cloned.1.call-update) | async-done | bytes 8388624 | tf_op jit(solution)/shard_map/all_gather | solution.py:61
  137.3 7.6 copy.24
  144.9 3.6 fusion.137
  148.6 1.0 copy-done
  149.6 3.3 fusion.138
  152.8 3.3 bitcast_add_fusion
  156.1 1.9 fusion.26
  158.1 2.3 pad_maximum_fusion
  160.5 42.7 %reduce-scatter.3.cloned.1.call-done = bf16[2,2,256,512]{3,2,0,1:T(8,128)(2,1)} async-done(((bf16[2,2,256,2048]{3,2,0,1:T(8,128)(2,1)}), bf16[2,2,256,512]{3,2,0,1:T(8,128)(2,1)}) %reduce-scatter.3.cloned.1.call-update) | async-done | bytes 1048592 | tf_op jit(solution)/shard_map/reduce_scatter | solution.py:103
  203.2 2.5 fusion.20
  206.2 34.1 %all-gather.10.cloned.1.call-done = bf16[2,2,256,2048]{3,2,0,1:T(8,128)(2,1)} async-done(((bf16[2,2,256,512]{3,2,0,1:T(8,128)(2,1)}), bf16[2,2,256,2048]{3,2,0,1:T(8,128)(2,1)}) %all-gather.10.cloned.1.call-update) | async-done | bytes 4194320 | tf_op jit(solution)/shard_map/all_gather | solution.py:108
  240.3 17.6 %fusion.45 = f32[2,256,512]{2,1,0:T(8,128)S(1)} fusion(s32[512]{0:T(512)S(1)} %iota_add_fusion, bf16[2,2,256,2048]{3,2,0,1:T(8,128)(2,1)} %all-gather.10.cloned.1.call-done), kind=kOutput, calls=%fused_computation.87 | convolution fusion | flops 1090519040 | bytes 3147776 | tf_op jit(solution)/shard_map/fmn,nc->fmc/dot_general | solution.py:30
  257.9 15.9 %fusion.47 = f32[2,256,512]{2,1,0:T(8,128)S(1)} fusion(s32[512]{0:T(512)S(1)} %iota_add_fusion, bf16[2,2,256,2048]{3,2,0,1:T(8,128)(2,1)S(1)} %copy-done.13), kind=kOutput, calls=%fused_computation.88 | convolution fusion | flops 1090519040 | bytes 3147776 | tf_op jit(solution)/shard_map/fmn,nc->fmc/dot_general | solution.py:30
  273.7 16.4 %fusion.124 = bf16[2,1,256,512]{3,2,0,1:T(8,128)(2,1)S(1)} fusion(f32[2,256,512]{2,1,0:T(8,128)S(1)} %fusion.45, s32[512]{0:T(512)S(1)} %iota_add_fusion, bf16[2,2,256,2048]{3,2,0,1:T(8,128)(2,1)S(1)} %copy-done.13), kind=kOutput, calls=%fused_computation.129 | convolution fusion | flops 1091043328 | bytes 3672064 | tf_op jit(solution)/shard_map/fmn,nc->fmc/dot_general | solution.py:30
  290.1 16.6 %fusion.121 = bf16[2,1,256,512]{3,2,0,1:T(8,128)(2,1)S(1)} fusion(f32[2,256,512]{2,1,0:T(8,128)S(1)} %fusion.47, s32[512]{0:T(512)S(1)} %iota_add_fusion, bf16[2,2,256,2048]{3,2,0,1:T(8,128)(2,1)S(1)} %copy-done.13), kind=kOutput, calls=%fused_computation.128 | convolution fusion | flops 1091043328 | bytes 3672064 | tf_op jit(solution)/shard_map/fmn,nc->fmc/dot_general | solution.py:30
  306.7 1.1 pad_maximum_fusion.3
  307.9 124.5 %all-gather.12.cloned.1.call-done = bf16[2,2,2048,512]{3,2,0,1:T(8,128)(2,1)} async-done(((bf16[2,2,256,512]{3,2,0,1:T(8,128)(2,1)}), bf16[2,2,2048,512]{3,2,0,1:T(8,128)(2,1)}) %all-gather.12.cloned.1.call-update) | async-done | bytes 8388624 | tf_op jit(solution)/shard_map/all_gather | solution.py:110
  432.4 10.8 fusion.6
  443.2 8.5 fusion.7
  451.7 8.7 fusion.92
  460.5 8.4 fusion.90
  470.4 38.3 %pmax.14 = f32[2]{0:T(128)S(1)} all-reduce(f32[2]{0:T(128)S(1)} %fusion.160), channel_id=1, replica_groups=mesh['src'=8,'rcv'=4] {'src','rcv'}, use_global_device_ids=true, to_apply=%region_2.3 | all-reduce | flops 2 | bytes 16 | tf_op jit(solution)/shard_map/pmax | solution.py:114
  509.3 1.0 copy-done.2
  510.3 2.8 multiply_convert_fusion.6
  513.3 125.6 %all-gather.14.cloned.1.call-done = bf16[2,2,2048,512]{2,3,0,1:T(8,128)(2,1)} async-done(((bf16[2,2,256,512]{2,3,0,1:T(8,128)(2,1)}), bf16[2,2,2048,512]{2,3,0,1:T(8,128)(2,1)}) %all-gather.14.cloned.1.call-update) | async-done | bytes 8388624 | tf_op jit(solution)/shard_map/all_gather | solution.py:80
  638.9 11.0 fusion.10
  649.9 8.7 fusion.11
  658.6 9.0 fusion.134
  667.6 8.6 fusion.133
  676.2 1.1 pad_maximum_fusion.4
  677.6 32.6 %all-gather.16.cloned.1.call-done = bf16[2,2,256,2048]{2,3,0,1:T(8,128)(2,1)} async-done(((bf16[2,2,256,512]{2,3,0,1:T(8,128)(2,1)}), bf16[2,2,256,2048]{2,3,0,1:T(8,128)(2,1)}) %all-gather.16.cloned.1.call-update) | async-done | bytes 4194320 | tf_op jit(solution)/shard_map/all_gather | solution.py:83
  710.1 18.5 %fusion.41 = f32[2,256,512]{2,1,0:T(8,128)S(1)} fusion(s32[512]{0:T(512)S(1)} %iota_add_fusion, bf16[2,2,256,2048]{2,3,0,1:T(8,128)(2,1)} %all-gather.16.cloned.1.call-done), kind=kOutput, calls=%fused_computation.85 | convolution fusion | flops 1090519040 | bytes 3147776 | tf_op jit(solution)/shard_map/fmn,nc->fmc/dot_general | solution.py:30
  728.6 16.9 %fusion.43 = f32[2,256,512]{2,1,0:T(8,128)S(1)} fusion(s32[512]{0:T(512)S(1)} %iota_add_fusion, bf16[2,2,256,2048]{2,3,0,1:T(8,128)(2,1)S(1)} %copy-done.16), kind=kOutput, calls=%fused_computation.86 | convolution fusion | flops 1090519040 | bytes 3147776 | tf_op jit(solution)/shard_map/fmn,nc->fmc/dot_general | solution.py:30
  745.5 17.2 %fusion.118 = bf16[2,1,256,512]{3,2,0,1:T(8,128)(2,1)S(1)} fusion(f32[2,256,512]{2,1,0:T(8,128)S(1)} %fusion.41, s32[512]{0:T(512)S(1)} %iota_add_fusion, bf16[2,2,256,2048]{2,3,0,1:T(8,128)(2,1)S(1)} %copy-done.16), kind=kOutput, calls=%fused_computation.127 | convolution fusion | flops 1091043328 | bytes 3672064 | tf_op jit(solution)/shard_map/fmn,nc->fmc/dot_general | solution.py:30
  762.8 16.8 %fusion.115 = bf16[2,1,256,512]{3,2,0,1:T(8,128)(2,1)S(1)} fusion(f32[2,256,512]{2,1,0:T(8,128)S(1)} %fusion.43, s32[512]{0:T(512)S(1)} %iota_add_fusion, bf16[2,2,256,2048]{2,3,0,1:T(8,128)(2,1)S(1)} %copy-done.16), kind=kOutput, calls=%fused_computation.126 | convolution fusion | flops 1091043328 | bytes 3672064 | tf_op jit(solution)/shard_map/fmn,nc->fmc/dot_general | solution.py:30
  779.6 1.1 pad_maximum_fusion.5
  780.8 34.6 %all-gather.18.cloned.1.call-done = bf16[2,2,256,2048]{3,2,0,1:T(8,128)(2,1)} async-done(((bf16[2,2,256,512]{3,2,0,1:T(8,128)(2,1)}), bf16[2,2,256,2048]{3,2,0,1:T(8,128)(2,1)}) %all-gather.18.cloned.1.call-update) | async-done | bytes 4194320 | tf_op jit(solution)/shard_map/all_gather | solution.py:86
  815.4 4.2 fusion.63
  819.6 3.6 fusion.62
  823.4 1.2 fusion.93
  824.6 1.4 subtract_bitcast_fusion
  826.9 1.3 fusion.135
  828.2 3.2 fusion.136
  831.4 1.3 convolution_subtract_fusion
  832.7 3.9 fusion.31
  836.6 2.3 pad_maximum_fusion.1
  838.9 44.5 %reduce-scatter.5.cloned.1.call-done = bf16[2,2,256,512]{3,2,0,1:T(8,128)(2,1)} async-done(((bf16[2,2,256,2048]{3,2,0,1:T(8,128)(2,1)}), bf16[2,2,256,512]{3,2,0,1:T(8,128)(2,1)}) %reduce-scatter.5.cloned.1.call-update) | async-done | bytes 1048592 | tf_op jit(solution)/shard_map/reduce_scatter | solution.py:103
  883.4 2.5 subtract_convert_fusion.2
  886.4 34.2 %all-gather.20.cloned.1.call-done = bf16[2,2,256,2048]{3,2,0,1:T(8,128)(2,1)} async-done(((bf16[2,2,256,512]{3,2,0,1:T(8,128)(2,1)}), bf16[2,2,256,2048]{3,2,0,1:T(8,128)(2,1)}) %all-gather.20.cloned.1.call-update) | async-done | bytes 4194320 | tf_op jit(solution)/shard_map/all_gather | solution.py:108
  920.6 17.6 %fusion.37 = f32[2,256,512]{2,1,0:T(8,128)S(1)} fusion(s32[512]{0:T(512)S(1)} %iota_add_fusion, bf16[2,2,256,2048]{3,2,0,1:T(8,128)(2,1)} %all-gather.20.cloned.1.call-done), kind=kOutput, calls=%fused_computation.83 | convolution fusion | flops 1090519040 | bytes 3147776 | tf_op jit(solution)/shard_map/fmn,nc->fmc/dot_general | solution.py:30
  938.2 15.9 %fusion.39 = f32[2,256,512]{2,1,0:T(8,128)S(1)} fusion(s32[512]{0:T(512)S(1)} %iota_add_fusion, bf16[2,2,256,2048]{3,2,0,1:T(8,128)(2,1)S(1)} %copy-done.15), kind=kOutput, calls=%fused_computation.84 | convolution fusion | flops 1090519040 | bytes 3147776 | tf_op jit(solution)/shard_map/fmn,nc->fmc/dot_general | solution.py:30
  954.0 16.4 %fusion.130 = bf16[2,1,256,512]{3,2,0,1:T(8,128)(2,1)S(1)} fusion(f32[2,256,512]{2,1,0:T(8,128)S(1)} %fusion.37, s32[512]{0:T(512)S(1)} %iota_add_fusion, bf16[2,2,256,2048]{3,2,0,1:T(8,128)(2,1)S(1)} %copy-done.15), kind=kOutput, calls=%fused_computation.131 | convolution fusion | flops 1091043328 | bytes 3672064 | tf_op jit(solution)/shard_map/fmn,nc->fmc/dot_general | solution.py:30
  970.4 17.0 %fusion.127 = bf16[2,1,256,512]{3,2,0,1:T(8,128)(2,1)S(1)} fusion(f32[2,256,512]{2,1,0:T(8,128)S(1)} %fusion.39, s32[512]{0:T(512)S(1)} %iota_add_fusion, bf16[2,2,256,2048]{3,2,0,1:T(8,128)(2,1)S(1)} %copy-done.15), kind=kOutput, calls=%fused_computation.130 | convolution fusion | flops 1091043328 | bytes 3672064 | tf_op jit(solution)/shard_map/fmn,nc->fmc/dot_general | solution.py:30
  987.4 1.2 pad_maximum_fusion.6
  988.6 42.2 %all-reduce = (f32[2]{0:T(128)S(1)}, f32[2]{0:T(128)S(1)}) all-reduce(f32[2]{0:T(128)S(1)} %get-tuple-element.7, f32[2]{0:T(128)S(1)} %get-tuple-element.6), channel_id=1, replica_groups=mesh['src'=8,'rcv'=4] {'src','rcv'}, use_global_device_ids=true, to_apply=%region_9.10 | all-reduce | flops 4 | bytes 32 | tf_op jit(solution)/shard_map/psum | solution.py:94
  1030.8 83.5 %all-gather.22.cloned.1.call-done = bf16[2,2,2048,512]{3,2,0,1:T(8,128)(2,1)} async-done(((bf16[2,2,256,512]{3,2,0,1:T(8,128)(2,1)}), bf16[2,2,2048,512]{3,2,0,1:T(8,128)(2,1)}) %all-gather.22.cloned.1.call-update) | async-done | bytes 8388624 | tf_op jit(solution)/shard_map/all_gather | solution.py:110
  1114.3 10.8 fusion.14
  1125.1 8.5 fusion.15
  1133.6 8.6 fusion.86
  1142.2 8.4 fusion.84
  1152.2 38.3 %pmax.15 = f32[2]{0:T(128)S(1)} all-reduce(f32[2]{0:T(128)S(1)} %fusion.161), channel_id=1, replica_groups=mesh['src'=8,'rcv'=4] {'src','rcv'}, use_global_device_ids=true, to_apply=%region_5.6 | all-reduce | flops 2 | bytes 16 | tf_op jit(solution)/shard_map/pmax | solution.py:114
  1191.1 2.6 broadcast_multiply_fusion
  1193.6 1.8 copy.39
  (71 shorter events, 7.6 us)
Async XLA Ops:
  7.2 130.2 %all-gather.24.cloned.1.call-start = ((), (), s32[]{:S(2)}) async-start(), calls=%async_computation.11 | async-start | bytes 9437184 | tf_op jit(solution)/shard_map/all_gather | solution.py:61
  7.9 195.3 %reduce-scatter.3.cloned.1.call-start = ((), (), s32[]{:S(2)}) async-start(), calls=%async_computation.2 | async-start | bytes 5242880 | tf_op jit(solution)/shard_map/reduce_scatter | solution.py:103
  137.3 7.6 copy-start.1
  144.9 4.6 copy-start
  160.4 79.8 %all-gather.10.cloned.1.call-start = ((), (), s32[]{:S(2)}) async-start(), calls=%async_computation.3 | async-start | bytes 5242880 | tf_op jit(solution)/shard_map/all_gather | solution.py:108
  205.7 226.7 %all-gather.12.cloned.1.call-start = ((), (), s32[]{:S(2)}) async-start(), calls=%async_computation.4 | async-start | bytes 9437184 | tf_op jit(solution)/shard_map/all_gather | solution.py:110
  240.3 17.6 %copy-start.13 = (bf16[2,2,256,2048]{3,2,0,1:T(8,128)(2,1)S(1)}, bf16[2,2,256,2048]{3,2,0,1:T(8,128)(2,1)}, u32[]{:S(2)}) copy-start(bf16[2,2,256,2048]{3,2,0,1:T(8,128)(2,1)} %all-gather.10.cloned.1.call-done) | copy-start | bytes 12582916
  307.8 331.1 %all-gather.14.cloned.1.call-start = ((), (), s32[]{:S(2)}) async-start(), calls=%async_computation.5 | async-start | bytes 9437184 | tf_op jit(solution)/shard_map/all_gather | solution.py:80
  432.4 10.8 copy-start.10
  460.5 8.4 copy-start.4
  468.9 1.0 copy-start.6
  509.3 1.0 copy-start.2
  513.1 197.1 %all-gather.16.cloned.1.call-start = ((), (), s32[]{:S(2)}) async-start(), calls=%async_computation.6 | async-start | bytes 5242880 | tf_op jit(solution)/shard_map/all_gather | solution.py:83
  638.9 11.0 copy-start.12
  677.3 138.0 %all-gather.18.cloned.1.call-start = ((), (), s32[]{:S(2)}) async-start(), calls=%async_computation.7 | async-start | bytes 5242880 | tf_op jit(solution)/shard_map/all_gather | solution.py:86
  710.1 18.5 %copy-start.16 = (bf16[2,2,256,2048]{2,3,0,1:T(8,128)(2,1)S(1)}, bf16[2,2,256,2048]{2,3,0,1:T(8,128)(2,1)}, u32[]{:S(2)}) copy-start(bf16[2,2,256,2048]{2,3,0,1:T(8,128)(2,1)} %all-gather.16.cloned.1.call-done) | copy-start | bytes 12582916
  780.8 102.7 %reduce-scatter.5.cloned.1.call-start = ((), (), s32[]{:S(2)}) async-start(), calls=%async_computation.8 | async-start | bytes 5242880 | tf_op jit(solution)/shard_map/reduce_scatter | solution.py:103
  815.4 4.2 copy-start.14
  815.4 7.8 slice-start
  819.6 3.8 slice-start.1
  838.9 81.7 %all-gather.20.cloned.1.call-start = ((), (), s32[]{:S(2)}) async-start(), calls=%async_computation.9 | async-start | bytes 5242880 | tf_op jit(solution)/shard_map/all_gather | solution.py:108
  886.0 228.3 %all-gather.22.cloned.1.call-start = ((), (), s32[]{:S(2)}) async-start(), calls=%async_computation.10 | async-start | bytes 9437184 | tf_op jit(solution)/shard_map/all_gather | solution.py:110
  920.6 17.6 %copy-start.15 = (bf16[2,2,256,2048]{3,2,0,1:T(8,128)(2,1)S(1)}, bf16[2,2,256,2048]{3,2,0,1:T(8,128)(2,1)}, u32[]{:S(2)}) copy-start(bf16[2,2,256,2048]{3,2,0,1:T(8,128)(2,1)} %all-gather.20.cloned.1.call-done) | copy-start | bytes 12582916
  1114.3 10.8 copy-start.11
  1142.2 8.5 copy-start.8
  1142.2 8.5 copy-start.3
  1142.2 8.5 copy-start.5
  1142.2 8.5 copy-start.7
  1150.7 1.0 copy-start.9
Sparse Core Ops, SparseCore 0:
  10.1 127.1 all-gather.23
  160.6 42.5 reduce-scatter.2
  205.8 34.4 all-gather.9
  307.9 124.4 all-gather.11
  513.2 125.6 all-gather.13
  677.5 32.6 all-gather.15
  780.9 34.4 all-gather.17
  839.0 44.3 reduce-scatter.4
  886.1 34.4 all-gather.19
  988.8 125.4 all-gather.21
